TPU v7x, 32 devices: a whole 2x2x4 slice. The times are simulated.
32 devices in a mesh: groups: 2 (over x), ctx: 16 (over z, y, core).
Axes of the slice: x: 2, y: 2, z: 4, core: 2. Of those that a mesh axis runs over, the one named last changes fastest.
Arguments:
- queries: bfloat16 [256, 2048], P(('groups', 'ctx')), parts along dimension 0, may hold values from -200 to 200
- slab_keys: bfloat16 [256, 2048], P(('groups', 'ctx')), parts along dimension 0, may hold values from -6 to 6
- slab_values: bfloat16 [256, 2048], P(('groups', 'ctx')), parts along dimension 0, may hold values from -6 to 6
- cache_keys: bfloat16 [16384, 2048], P(('groups', 'ctx')), parts along dimension 0, may hold values from -12 to 12
- cache_values: bfloat16 [16384, 2048], P(('groups', 'ctx')), parts along dimension 0, may hold values from -6 to 6
- offset: int32 [2], P('groups'), parts along dimension 0, may hold values from 2048 to 8192
- slab_len: int32 [2], P('groups'), parts along dimension 0, may hold values from 64 to 128
Outputs:
- attended: bfloat16 [256, 2048], P(('groups', 'ctx')), parts along dimension 0
There are 2 independent parts, one for each index of `groups`. A program takes and returns all parts, laid end to end along the dimension named above; each array names one. Nothing has to cross between parts.
All inputs are finite; a program needn't handle non-finite values.
Results may differ from a plain program's by a relative error of at most 0.0081.
Values may be sent and summed in bfloat16 or wider, within the bound.
A program may use at most 128 MiB of HBM per device.

v0:
```python
import jax
import jax.numpy as jnp
from jax import lax
from jax.sharding import PartitionSpec as P

DH = 128
KB = 256
very_low = -1e30


def block_state(query_heads, key_blocks, value_blocks, visible, score_scale):
    scores = (
        jnp.einsum("qhd,gkhd->qghk", query_heads, key_blocks, preferred_element_type=jnp.float32)
        * score_scale
    )
    visible_head = visible[:, :, None, :]
    masked = jnp.where(visible_head, scores, very_low)
    maxima = jnp.max(masked, axis=3)
    weights = jnp.exp(jnp.where(visible_head, scores - maxima[..., None], -jnp.inf))
    totals = jnp.sum(weights, axis=3)
    rounded = weights.astype(jnp.bfloat16)
    products = jnp.einsum(
        "qghk,gkhd->qghd", rounded, value_blocks, preferred_element_type=jnp.float32
    )
    return (maxima, totals, products)


def absorb(running, terms):
    largest, weight_sum, weighted = running
    maxima, totals, products = terms
    new_largest = jnp.maximum(largest, jnp.max(maxima, axis=1))
    old_factor = jnp.exp(largest - new_largest)
    factors = jnp.exp(maxima - new_largest[:, None, :])
    weight_sum = weight_sum * old_factor + jnp.sum(factors * totals, axis=1)
    weighted = weighted * old_factor[..., None] + jnp.sum(factors[..., None] * products, axis=1)
    return (new_largest, weight_sum, weighted)


def body(queries, slab_keys, slab_values, cache_keys, cache_values, offset, slab_len):
    device_rank = lax.axis_index("ctx")
    device_count = lax.axis_size("ctx")
    own_rows = queries.shape[0]
    slab_rows = own_rows * device_count
    cache_rows = cache_keys.shape[0]
    head_count = queries.shape[1] // DH
    score_scale = DH ** (-0.5)
    gathered = lax.all_gather(queries, "ctx", axis=0, tiled=True)
    query_heads = gathered.reshape(slab_rows, head_count, DH)
    running = (
        jnp.full((slab_rows, head_count), very_low, jnp.float32),
        jnp.zeros((slab_rows, head_count), jnp.float32),
        jnp.zeros((slab_rows, head_count, DH), jnp.float32),
    )
    for block_number in range(cache_rows // KB):
        block_start = block_number * KB
        key_blocks = cache_keys[block_start : block_start + KB].reshape(1, KB, head_count, DH)
        value_blocks = cache_values[block_start : block_start + KB].reshape(1, KB, head_count, DH)
        positions = device_rank * cache_rows + block_start + jnp.arange(KB, dtype=jnp.int32)
        visible = jnp.broadcast_to((positions < offset[0])[None, None, :], (slab_rows, 1, KB))
        running = absorb(
            running, block_state(query_heads, key_blocks, value_blocks, visible, score_scale)
        )
    own_index = device_rank * own_rows + jnp.arange(own_rows, dtype=jnp.int32)
    largest, weight_sum, weighted = running
    quotient = (weighted / jnp.maximum(weight_sum, 1.0)[..., None]).astype(jnp.bfloat16)
    parts_quotient = lax.all_to_all(
        quotient.reshape(1, slab_rows, head_count * DH),
        "ctx",
        split_axis=1,
        concat_axis=0,
        tiled=True,
    )
    parts_sum, parts_largest = (
        lax.all_to_all(weight_sum[None], "ctx", split_axis=1, concat_axis=0, tiled=True),
        lax.all_to_all(largest[None], "ctx", split_axis=1, concat_axis=0, tiled=True),
    )
    own_largest = jnp.max(parts_largest, axis=0)
    factors = jnp.exp(parts_largest - own_largest[None]) * parts_sum
    own_sum = jnp.sum(factors, axis=0)
    own_weighted = jnp.sum(
        factors[..., None]
        * parts_quotient.reshape(device_count, own_rows, head_count, DH).astype(jnp.float32),
        axis=0,
    )
    own_state = (own_largest, own_sum, own_weighted)
    own_queries = queries.reshape(own_rows, head_count, DH)
    keys_piece = lax.all_gather(slab_keys, "ctx", axis=0, tiled=True)
    values_piece = lax.all_gather(slab_values, "ctx", axis=0, tiled=True)
    piece_rows = keys_piece.shape[0]
    piece_blocks = piece_rows // own_rows
    key_index = jnp.arange(piece_rows, dtype=jnp.int32).reshape(piece_blocks, own_rows)
    visible = (key_index[None] <= own_index[:, None, None]) & (key_index[None] < slab_len[0])
    own_state = absorb(
        own_state,
        block_state(
            own_queries,
            keys_piece.reshape(piece_blocks, own_rows, head_count, DH),
            values_piece.reshape(piece_blocks, own_rows, head_count, DH),
            visible,
            score_scale,
        ),
    )
    final_largest, final_sum, final_weighted = own_state
    combined = (final_weighted / final_sum[..., None]).reshape(own_rows, head_count * DH)
    combined = jnp.where((own_index < slab_len[0])[:, None], combined, 0.0)
    return combined.astype(jnp.bfloat16)


def solution(mesh):
    placed = (
        P(("groups", "ctx"), None),
        P(("groups", "ctx"), None),
        P(("groups", "ctx"), None),
        P(("groups", "ctx"), None),
        P(("groups", "ctx"), None),
        P("groups"),
        P("groups"),
    )
    return jax.shard_map(
        body, mesh=mesh, in_specs=placed, out_specs=P(("groups", "ctx"), None), check_vma=False
    )
```

profile of v0, /device:TPU:0, one launch (start us, length us, event | category | flops | bytes accessed | tf_op | source)
XLA Modules:
  0.0 140.0 jit_solution(13504468689925622335)
XLA Ops:
  0.7 1.7 %fusion.59 = (bf16[256,2048]{1,0:T(8,128)(2,1)S(1)}, bf16[256,2048]{1,0:T(8,128)(2,1)S(1)}) fusion(bf16[512,2048]{1,0:T(8,128)(2,1)} %param.10), kind=kLoop, calls=%fused_computation.94 | loop fusion | bytes 4194304 | tf_op jit(solution)/shard_map/slice | solution.py:56
  3.1 24.6 %all_gather.9 = bf16[128,2048]{1,0:T(8,128)(2,1)S(1)} all-gather(bf16[8,2048]{1,0:T(8,128)(2,1)S(1)} %copy-done.5), channel_id=1, replica_groups=mesh['groups'=2,'ctx'=16] {'ctx'}, dimensions={0}, use_global_device_ids=true | all-gather | bytes 557056 | tf_op jit(solution)/shard_map/all_gather | solution.py:47
  28.0 1.3 copy.96
  29.3 0.6 fusion.3
  30.5 0.6 fusion
  32.3 0.7 reduce.7
  33.0 0.7 reshape.418
  33.7 3.5 %all-to-all-start = ((f32[16,1,128]{2,1,0:T(1,128)}), f32[16,1,128]{2,1,0:T(1,128)S(1)}, u32[]{:S(2)}, u32[]{:S(2)}) async-start(f32[16,1,128]{2,1,0:T(1,128)} %reshape.418), calls=%async_computation | async-start | bytes 16384 | tf_op jit(solution)/shard_map/all_to_all | solution.py:75
  37.9 23.2 %all_gather.10 = bf16[128,2048]{1,0:T(8,128)(2,1)S(1)} all-gather(bf16[8,2048]{1,0:T(8,128)(2,1)S(1)} %copy-done.4), channel_id=1, replica_groups=mesh['groups'=2,'ctx'=16] {'ctx'}, dimensions={0}, use_global_device_ids=true | all-gather | bytes 557056 | tf_op jit(solution)/shard_map/all_gather | solution.py:87
  61.2 0.9 copy.112
  62.1 3.1 %fusion.58 = (bf16[256,2048]{1,0:T(8,128)(2,1)}, bf16[256,2048]{1,0:T(8,128)(2,1)}) fusion(bf16[512,2048]{1,0:T(8,128)(2,1)} %param.11), kind=kLoop, calls=%fused_computation.93 | loop fusion | bytes 4194304 | tf_op jit(solution)/shard_map/slice | solution.py:57
  65.1 1.5 %copy.71 = bf16[256,2048]{0,1:T(8,128)(2,1)S(1)} copy(bf16[256,2048]{1,0:T(8,128)(2,1)} %get-tuple-element.16) | data formatting | bytes 2097152 | tf_op jit(solution)/shard_map/slice | solution.py:57
  66.6 3.3 %fusion.12 = f32[128,1,16,128]{0,3,2,1:T(8,128)} fusion(bf16[256,16,128]{0,2,1:T(8,128)(2,1)S(1)} %bitcast.143, f32[16,256,128]{2,1,0:T(8,128)} %copy-done, f32[128,16]{0,1:T(8,128)S(1)} %get-tuple-element.29, pred[256]{0:T(512)(128)(4,1)S(1)} %get-tuple-element.32, f32[128,16]{0,1:T(8,128)S(1)} %get-tuple-element.23), kind=kOutput, calls=%fused_computation.20 | convolution fusion | flops 136577024 | bytes 4210944 | tf_op jit(solution)/shard_map/qghk,gkhd->qghd/dot_general | solution.py:22
  69.9 3.6 %copy.73 = f32[1,128,2048]{2,0,1:T(1,128)} copy(f32[1,128,2048]{1,2,0:T(8,128)} %bitcast.144) | data formatting | bytes 2097152 | tf_op jit(solution)/shard_map/reduce_sum | solution.py:35
  73.6 1.5 %copy.75 = bf16[256,2048]{0,1:T(8,128)(2,1)S(1)} copy(bf16[256,2048]{1,0:T(8,128)(2,1)} %get-tuple-element.17) | data formatting | bytes 2097152 | tf_op jit(solution)/shard_map/slice | solution.py:57
  75.0 1.8 %fusion.13 = f32[128,1,16,128]{0,3,2,1:T(8,128)} fusion(bf16[256,16,128]{0,2,1:T(8,128)(2,1)S(1)} %bitcast.145, f32[16,256,128]{2,1,0:T(8,128)S(1)} %get-tuple-element.28, f32[128,16]{0,1:T(8,128)S(1)} %get-tuple-element.27, pred[256]{0:T(512)(128)(4,1)S(1)} %get-tuple-element.31, f32[128,16]{0,1:T(8,128)S(1)} %get-tuple-element.15), kind=kOutput, calls=%fused_computation.21 | convolution fusion | flops 136577024 | bytes 4210944 | tf_op jit(solution)/shard_map/qghk,gkhd->qghd/dot_general | solution.py:22
  76.8 2.5 %copy.77 = f32[1,128,2048]{2,0,1:T(1,128)S(1)} copy(f32[1,128,2048]{1,2,0:T(8,128)} %bitcast.146) | data formatting | bytes 2097152 | tf_op jit(solution)/shard_map/reduce_sum | solution.py:35
  81.5 3.3 %fusion.60 = bf16[128,1,2048]{2,1,0:T(2,128)(2,1)S(1)} fusion(f32[1,128,2048]{2,0,1:T(1,128)S(1)} %bitcast.152, f32[1,128,2048]{2,0,1:T(1,128)S(1)} %copy.77, f32[1,128,2048]{2,0,1:T(1,128)S(1)} %bitcast.151, f32[1,128,2048]{2,0,1:T(1,128)S(1)} %bitcast.150, f32[1,128,2048]{2,0,1:T(1,128)S(1)} %copy-done.1), kind=kLoop, calls=%fused_computation.96 | loop fusion | flops 1310720 | bytes 5767168
  84.8 0.6 fusion.28
  85.5 0.7 reduce.10
  86.2 0.7 reshape.422
  86.9 3.5 %all-to-all-start.1 = ((f32[16,1,128]{2,1,0:T(1,128)}), f32[16,1,128]{2,1,0:T(1,128)S(1)}, u32[]{:S(2)}, u32[]{:S(2)}) async-start(f32[16,1,128]{2,1,0:T(1,128)} %reshape.422), calls=%async_computation.1 | async-start | bytes 16384 | tf_op jit(solution)/shard_map/all_to_all | solution.py:74
  90.4 23.4 %all_gather.11 = bf16[128,2048]{1,0:T(8,128)(2,1)S(1)} all-gather(bf16[8,2048]{1,0:T(8,128)(2,1)S(1)} %copy-done.6), channel_id=1, replica_groups=mesh['groups'=2,'ctx'=16] {'ctx'}, dimensions={0}, use_global_device_ids=true | all-gather | bytes 557056 | tf_op jit(solution)/shard_map/all_gather | solution.py:88
  114.4 3.7 %reduce.9 = bf16[128,2048]{1,0:T(8,128)(2,1)S(1)} reduce(bf16[128,1,2048]{2,1,0:T(2,128)(2,1)S(1)} %fusion.60, bf16[]{:T(256)} %broadcast.196), dimensions={1}, to_apply=%fusion.60.reduce_sub_computation | reduce | bytes 1048578
  118.1 1.3 reshape.420
  119.4 3.6 %all-to-all-start.2 = ((bf16[16,2,8192]{2,1,0:T(2,128)(2,1)}), bf16[16,2,8192]{2,1,0:T(2,128)(2,1)S(1)}, u32[]{:S(2)}, u32[]{:S(2)}) async-start(bf16[16,2,8192]{2,1,0:T(2,128)(2,1)} %reshape.420), calls=%async_computation.2 | async-start | bytes 1048576 | tf_op jit(solution)/shard_map/all_to_all | solution.py:66
  123.0 0.6 reduce.8
  123.8 0.6 reduce.11
  124.8 0.6 fusion.14
  125.4 11.8 %all-to-all-done.2 = bf16[16,2,8192]{2,1,0:T(2,128)(2,1)S(1)} async-done(((bf16[16,2,8192]{2,1,0:T(2,128)(2,1)}), bf16[16,2,8192]{2,1,0:T(2,128)(2,1)S(1)}, u32[]{:S(2)}, u32[]{:S(2)}) %all-to-all-start.2) | async-done | bytes 524320 | tf_op jit(solution)/shard_map/all_to_all | solution.py:66
  137.8 1.1 bitcast_convert_fusion
  139.3 0.7 fusion.33
  (53 shorter events, 7.3 us)
Async XLA Ops:
  2.3 0.8 copy-start.5
  29.3 1.2 copy-start.2
  29.9 1.4 copy-start
  31.3 6.7 %copy-start.4 = (bf16[8,2048]{1,0:T(8,128)(2,1)S(1)}, bf16[8,2048]{1,0:T(8,128)(2,1)}, u32[]{:S(2)}) copy-start(bf16[8,2048]{1,0:T(8,128)(2,1)} %param.8) | copy-start | bytes 98308
  33.7 53.2 %all-to-all-start = ((f32[16,1,128]{2,1,0:T(1,128)}), f32[16,1,128]{2,1,0:T(1,128)S(1)}, u32[]{:S(2)}, u32[]{:S(2)}) async-start(f32[16,1,128]{2,1,0:T(1,128)} %reshape.418), calls=%async_computation | async-start | bytes 16384 | tf_op jit(solution)/shard_map/all_to_all | solution.py:75
  76.8 2.9 %copy-start.3 = (bf16[16,8,16,128]{3,2,1,0:T(8,128)(2,1)S(1)}, bf16[16,8,16,128]{3,2,1,0:T(8,128)(2,1)}, u32[]{:S(2)}) copy-start(bf16[16,8,16,128]{3,2,1,0:T(8,128)(2,1)} %copy.112) | copy-start | bytes 1572868
  80.3 1.2 copy-start.1
  84.8 5.6 %copy-start.6 = (bf16[8,2048]{1,0:T(8,128)(2,1)S(1)}, bf16[8,2048]{1,0:T(8,128)(2,1)}, u32[]{:S(2)}) copy-start(bf16[8,2048]{1,0:T(8,128)(2,1)} %param.9) | copy-start | bytes 98308
  86.9 32.5 %all-to-all-start.1 = ((f32[16,1,128]{2,1,0:T(1,128)}), f32[16,1,128]{2,1,0:T(1,128)S(1)}, u32[]{:S(2)}, u32[]{:S(2)}) async-start(f32[16,1,128]{2,1,0:T(1,128)} %reshape.422), calls=%async_computation.1 | async-start | bytes 16384 | tf_op jit(solution)/shard_map/all_to_all | solution.py:74
  119.4 17.8 %all-to-all-start.2 = ((bf16[16,2,8192]{2,1,0:T(2,128)(2,1)}), bf16[16,2,8192]{2,1,0:T(2,128)(2,1)S(1)}, u32[]{:S(2)}, u32[]{:S(2)}) async-start(bf16[16,2,8192]{2,1,0:T(2,128)(2,1)} %reshape.420), calls=%async_computation.2 | async-start | bytes 1048576 | tf_op jit(solution)/shard_map/all_to_all | solution.py:66
where the time goes:
time: 141 us; the launch traced here: 140 us
  blocking collectives  71.2 us (50%)
  local copies, waits for them, and re-layouts  23.8 us (17%)
  other arithmetic  13.6 us (10%)
  waiting for transfers between devices  11.9 us (8%)
  starting transfers between devices  10.5 us (7%)
  matrix products  7.41 us (5%)
  between operations  1.62 us (1%)
    all_gather x1, blocking collectives, body(): gathered = lax.all_gather(queries, 'ctx', axis=0, tiled=True)  24.6 us
    all_gather x1, blocking collectives, body(): values_piece = lax.all_gather(slab_values, 'ctx', axis=0, tiled=True)  23.4 us
    all_gather x1, blocking collectives, body(): keys_piece = lax.all_gather(slab_keys, 'ctx', axis=0, tiled=True)  23.2 us
    all_to_all x1, waiting for transfers between devices, body(): lax.all_to_all(quotient.reshape(1, slab_rows, head_count * DH), 'ctx', sp...  11.8 us
    unnamed x5, other arithmetic  8.48 us
    unnamed x25, local copies, waits for them, and re-layouts  7.98 us
    reduce_sum x2, local copies, waits for them, and re-layouts, absorb(): jnp.sum(factors[..., None] * products, axis=1)  6.12 us
    slice x3, local copies, waits for them, and re-layouts, body(): cache_values[block_start:block_start + KB].reshape(1, KB, head_count, DH)  6.04 us
  transfers between devices with their start and end apart: 3, of which 1 were waited for; matrix products, arithmetic and copies ran while one was open for 24% of the time, Pallas kernels for 0%

commit v1 on v0

--- a/solution.py
+++ b/solution.py
@@ -85,7 +85,17 @@
     own_state = (own_largest, own_sum, own_weighted)
     own_queries = queries.reshape(own_rows, head_count, DH)
     keys_piece = lax.all_gather(slab_keys, "ctx", axis=0, tiled=True)
-    values_piece = lax.all_gather(slab_values, "ctx", axis=0, tiled=True)
+    length, here, extent = (lax.axis_size("ctx"), lax.axis_index("ctx"), slab_values.shape[0])
+    ahead = [(i, (i + 1) % length) for i in range(length)]
+    values_piece = jnp.zeros(
+        (*slab_values.shape[:0], length * extent, *slab_values.shape[0 + 1 :]), slab_values.dtype
+    )
+    held = slab_values
+    for step in range(length):
+        holder = (here - step) % length
+        values_piece = lax.dynamic_update_slice_in_dim(values_piece, held, holder * extent, axis=0)
+        if step < length - 1:
+            held = lax.ppermute(held, "ctx", ahead)
     piece_rows = keys_piece.shape[0]
     piece_blocks = piece_rows // own_rows
     key_index = jnp.arange(piece_rows, dtype=jnp.int32).reshape(piece_blocks, own_rows)

time: 141 us -> 204 us (1.45)
  waiting for transfers between devices: 11.9 us -> 90.4 us
  blocking collectives: 71.2 us -> 47.6 us
  starting transfers between devices: 10.5 us -> 13.7 us
  local copies, waits for them, and re-layouts: 23.8 us -> 26.9 us
    ppermute x0 -> x15, waiting for transfers between devices: none -> 90.4 us  [body(): held = lax.ppermute(held, 'ctx', ahead)]
    all_gather x1 -> x0, blocking collectives: 23.4 us -> none  [body(): values_piece = lax.all_gather(slab_values, 'ctx', axis=0, tiled=True)]
    all_to_all x1, waiting for transfers between devices: 11.8 us -> 0.01 us  [body(): lax.all_to_all(quotient.reshape(1, slab_rows, head_count * DH), 'ctx', sp...]
    all_to_all x1, starting transfers between devices: 3.57 us -> 5.8 us  [body(): lax.all_to_all(quotient.reshape(1, slab_rows, head_count * DH), 'ctx', sp...]
    unnamed x25 -> x27, local copies, waits for them, and re-layouts: 7.98 us -> 7.88 us
  transfers between devices with their start and end apart: 3 -> 18, of which waited for: 1 -> 14; matrix products, arithmetic and copies ran while one was open for 24% -> 19% of each run, Pallas kernels for 0% -> 0%
where the time goes in v1:
time: 204 us; the launch traced here: 203 us
  waiting for transfers between devices  90.4 us (44%)
  blocking collectives  47.6 us (23%)
  local copies, waits for them, and re-layouts  26.9 us (13%)
  other arithmetic  15.4 us (8%)
  starting transfers between devices  13.7 us (7%)
  matrix products  7.41 us (4%)
    ppermute x15, waiting for transfers between devices, body(): held = lax.ppermute(held, 'ctx', ahead)  90.4 us
    all_gather x1, blocking collectives, body(): gathered = lax.all_gather(queries, 'ctx', axis=0, tiled=True)  24.6 us
    all_gather x1, blocking collectives, body(): keys_piece = lax.all_gather(slab_keys, 'ctx', axis=0, tiled=True)  23 us
    unnamed x5, other arithmetic  9.1 us
    unnamed x27, local copies, waits for them, and re-layouts  7.88 us
    reduce_sum x2, local copies, waits for them, and re-layouts, absorb(): jnp.sum(factors[..., None] * products, axis=1)  6.12 us
    slice x3, local copies, waits for them, and re-layouts, body(): cache_values[block_start:block_start + KB].reshape(1, KB, head_count, DH)  6.04 us
    all_to_all x1, starting transfers between devices, body(): lax.all_to_all(quotient.reshape(1, slab_rows, head_count * DH), 'ctx', sp...  5.8 us
  transfers between devices with their start and end apart: 18, of which 14 were waited for; matrix products, arithmetic and copies ran while one was open for 19% of the time, Pallas kernels for 0%

profile of v1, /device:TPU:0, one launch (start us, length us, event | category | flops | bytes accessed | tf_op | source)
XLA Modules:
  0.0 203.4 jit_solution(10085835974880276209)
XLA Ops:
  0.7 1.7 fusion.59
  3.1 24.6 %all_gather.6 = bf16[128,2048]{1,0:T(8,128)(2,1)S(1)} all-gather(bf16[8,2048]{1,0:T(8,128)(2,1)S(1)} %copy-done.6), channel_id=1, replica_groups=mesh['groups'=2,'ctx'=16] {'ctx'}, dimensions={0}, use_global_device_ids=true | all-gather | bytes 557056 | tf_op jit(solution)/shard_map/all_gather | solution.py:47
  28.0 1.3 copy.96
  34.4 3.5 %all-to-all-start = ((f32[16,1,128]{2,1,0:T(1,128)}), f32[16,1,128]{2,1,0:T(1,128)S(1)}, u32[]{:S(2)}, u32[]{:S(2)}) async-start(f32[16,1,128]{2,1,0:T(1,128)} %reshape.418), calls=%async_computation | async-start | bytes 16384 | tf_op jit(solution)/shard_map/all_to_all | solution.py:75
  38.9 23.0 %all_gather.7 = bf16[128,2048]{1,0:T(8,128)(2,1)S(1)} all-gather(bf16[8,2048]{1,0:T(8,128)(2,1)S(1)} %copy-done.5), channel_id=1, replica_groups=mesh['groups'=2,'ctx'=16] {'ctx'}, dimensions={0}, use_global_device_ids=true | all-gather | bytes 557056 | tf_op jit(solution)/shard_map/all_gather | solution.py:87
  62.9 3.1 %fusion.58 = (bf16[256,2048]{1,0:T(8,128)(2,1)}, bf16[256,2048]{1,0:T(8,128)(2,1)}) fusion(bf16[512,2048]{1,0:T(8,128)(2,1)} %param.11), kind=kLoop, calls=%fused_computation.109 | loop fusion | bytes 4194304 | tf_op jit(solution)/shard_map/slice | solution.py:57
  65.9 1.5 copy.71
  67.4 3.3 %fusion.12 = f32[128,1,16,128]{0,3,2,1:T(8,128)} fusion(bf16[256,16,128]{0,2,1:T(8,128)(2,1)S(1)} %bitcast.143, f32[16,256,128]{2,1,0:T(8,128)} %copy-done, f32[128,16]{0,1:T(8,128)S(1)} %get-tuple-element.29, pred[256]{0:T(512)(128)(4,1)S(1)} %get-tuple-element.32, f32[128,16]{0,1:T(8,128)S(1)} %get-tuple-element.23), kind=kOutput, calls=%fused_computation.20 | convolution fusion | flops 136577024 | bytes 4210944 | tf_op jit(solution)/shard_map/qghk,gkhd->qghd/dot_general | solution.py:22
  70.7 3.6 %copy.73 = f32[1,128,2048]{2,0,1:T(1,128)} copy(f32[1,128,2048]{1,2,0:T(8,128)} %bitcast.144) | data formatting | bytes 2097152 | tf_op jit(solution)/shard_map/reduce_sum | solution.py:35
  74.4 1.5 copy.75
  75.8 1.8 fusion.13
  77.6 2.5 %copy.77 = f32[1,128,2048]{2,0,1:T(1,128)S(1)} copy(f32[1,128,2048]{1,2,0:T(8,128)} %bitcast.146) | data formatting | bytes 2097152 | tf_op jit(solution)/shard_map/reduce_sum | solution.py:35
  83.5 1.2 div.29
  84.7 3.8 %fusion.60 = bf16[128,1,2048]{2,1,0:T(2,128)(2,1)S(1)} fusion(f32[1,128,2048]{2,0,1:T(1,128)S(1)} %bitcast.152, f32[1,128,2048]{2,0,1:T(1,128)S(1)} %copy.77, f32[1,128,2048]{2,0,1:T(1,128)S(1)} %bitcast.151, f32[1,128,2048]{2,0,1:T(1,128)S(1)} %bitcast.150, f32[1,128,2048]{2,0,1:T(1,128)S(1)} %copy-done.1), kind=kLoop, calls=%fused_computation.112 | loop fusion | flops 1310720 | bytes 5767168
  90.9 3.7 %all-to-all-start.1 = ((f32[16,1,128]{2,1,0:T(1,128)}), f32[16,1,128]{2,1,0:T(1,128)S(1)}, u32[]{:S(2)}, u32[]{:S(2)}) async-start(f32[16,1,128]{2,1,0:T(1,128)} %reshape.422), calls=%async_computation.1 | async-start | bytes 16384 | tf_op jit(solution)/shard_map/all_to_all | solution.py:74
  95.5 3.7 %reduce.9 = bf16[128,2048]{1,0:T(8,128)(2,1)S(1)} reduce(bf16[128,1,2048]{2,1,0:T(2,128)(2,1)S(1)} %fusion.60, bf16[]{:T(256)} %broadcast.212), dimensions={1}, to_apply=%fusion.60.reduce_sub_computation | reduce | bytes 1048578
  99.3 1.3 reshape.420
  101.4 5.8 %all-to-all-start.2 = ((bf16[16,2,8192]{2,1,0:T(2,128)(2,1)}), bf16[16,2,8192]{2,1,0:T(2,128)(2,1)S(1)}, u32[]{:S(2)}, u32[]{:S(2)}) async-start(bf16[16,2,8192]{2,1,0:T(2,128)(2,1)} %reshape.420), calls=%async_computation.2 | async-start | bytes 1048576 | tf_op jit(solution)/shard_map/all_to_all | solution.py:66
  109.5 12.1 %collective-permute-done.1 = bf16[8,2048]{1,0:T(8,128)(2,1)S(1)} collective-permute-done((bf16[8,2048]{1,0:T(8,128)(2,1)}, bf16[8,2048]{1,0:T(8,128)(2,1)S(1)}, u32[]{:S(2)}, u32[]{:S(2)}) %collective-permute-start.1) | collective-permute-done | bytes 32800 | tf_op jit(solution)/shard_map/ppermute | solution.py:98
  121.6 6.0 %collective-permute-done.2 = bf16[8,2048]{1,0:T(8,128)(2,1)S(1)} collective-permute-done((bf16[8,2048]{1,0:T(8,128)(2,1)S(1)}, bf16[8,2048]{1,0:T(8,128)(2,1)S(1)}, u32[]{:S(2)}, u32[]{:S(2)}) %collective-permute-start.2) | collective-permute-done | bytes 32800 | tf_op jit(solution)/shard_map/ppermute | solution.py:98
  127.6 6.0 %collective-permute-done.3 = bf16[8,2048]{1,0:T(8,128)(2,1)S(1)} collective-permute-done((bf16[8,2048]{1,0:T(8,128)(2,1)S(1)}, bf16[8,2048]{1,0:T(8,128)(2,1)S(1)}, u32[]{:S(2)}, u32[]{:S(2)}) %collective-permute-start.3) | collective-permute-done | bytes 32800 | tf_op jit(solution)/shard_map/ppermute | solution.py:98
  133.6 6.0 %collective-permute-done.4 = bf16[8,2048]{1,0:T(8,128)(2,1)S(1)} collective-permute-done((bf16[8,2048]{1,0:T(8,128)(2,1)S(1)}, bf16[8,2048]{1,0:T(8,128)(2,1)S(1)}, u32[]{:S(2)}, u32[]{:S(2)}) %collective-permute-start.4) | collective-permute-done | bytes 32800 | tf_op jit(solution)/shard_map/ppermute | solution.py:98
  139.7 6.0 %collective-permute-done.5 = bf16[8,2048]{1,0:T(8,128)(2,1)S(1)} collective-permute-done((bf16[8,2048]{1,0:T(8,128)(2,1)S(1)}, bf16[8,2048]{1,0:T(8,128)(2,1)S(1)}, u32[]{:S(2)}, u32[]{:S(2)}) %collective-permute-start.5) | collective-permute-done | bytes 32800 | tf_op jit(solution)/shard_map/ppermute | solution.py:98
  145.7 6.0 %collective-permute-done.6 = bf16[8,2048]{1,0:T(8,128)(2,1)S(1)} collective-permute-done((bf16[8,2048]{1,0:T(8,128)(2,1)S(1)}, bf16[8,2048]{1,0:T(8,128)(2,1)S(1)}, u32[]{:S(2)}, u32[]{:S(2)}) %collective-permute-start.6) | collective-permute-done | bytes 32800 | tf_op jit(solution)/shard_map/ppermute | solution.py:98
  151.8 6.0 %collective-permute-done.7 = bf16[8,2048]{1,0:T(8,128)(2,1)S(1)} collective-permute-done((bf16[8,2048]{1,0:T(8,128)(2,1)S(1)}, bf16[8,2048]{1,0:T(8,128)(2,1)S(1)}, u32[]{:S(2)}, u32[]{:S(2)}) %collective-permute-start.7) | collective-permute-done | bytes 32800 | tf_op jit(solution)/shard_map/ppermute | solution.py:98
  157.8 6.0 %collective-permute-done.8 = bf16[8,2048]{1,0:T(8,128)(2,1)S(1)} collective-permute-done((bf16[8,2048]{1,0:T(8,128)(2,1)S(1)}, bf16[8,2048]{1,0:T(8,128)(2,1)S(1)}, u32[]{:S(2)}, u32[]{:S(2)}) %collective-permute-start.8) | collective-permute-done | bytes 32800 | tf_op jit(solution)/shard_map/ppermute | solution.py:98
  163.8 6.0 %collective-permute-done.9 = bf16[8,2048]{1,0:T(8,128)(2,1)S(1)} collective-permute-done((bf16[8,2048]{1,0:T(8,128)(2,1)S(1)}, bf16[8,2048]{1,0:T(8,128)(2,1)S(1)}, u32[]{:S(2)}, u32[]{:S(2)}) %collective-permute-start.9) | collective-permute-done | bytes 32800 | tf_op jit(solution)/shard_map/ppermute | solution.py:98
  169.9 6.0 %collective-permute-done.10 = bf16[8,2048]{1,0:T(8,128)(2,1)S(1)} collective-permute-done((bf16[8,2048]{1,0:T(8,128)(2,1)S(1)}, bf16[8,2048]{1,0:T(8,128)(2,1)S(1)}, u32[]{:S(2)}, u32[]{:S(2)}) %collective-permute-start.10) | collective-permute-done | bytes 32800 | tf_op jit(solution)/shard_map/ppermute | solution.py:98
  175.9 6.0 %collective-permute-done.11 = bf16[8,2048]{1,0:T(8,128)(2,1)S(1)} collective-permute-done((bf16[8,2048]{1,0:T(8,128)(2,1)S(1)}, bf16[8,2048]{1,0:T(8,128)(2,1)S(1)}, u32[]{:S(2)}, u32[]{:S(2)}) %collective-permute-start.11) | collective-permute-done | bytes 32800 | tf_op jit(solution)/shard_map/ppermute | solution.py:98
  181.9 6.0 %collective-permute-done.12 = bf16[8,2048]{1,0:T(8,128)(2,1)S(1)} collective-permute-done((bf16[8,2048]{1,0:T(8,128)(2,1)S(1)}, bf16[8,2048]{1,0:T(8,128)(2,1)S(1)}, u32[]{:S(2)}, u32[]{:S(2)}) %collective-permute-start.12) | collective-permute-done | bytes 32800 | tf_op jit(solution)/shard_map/ppermute | solution.py:98
  188.0 6.0 %collective-permute-done.13 = bf16[8,2048]{1,0:T(8,128)(2,1)S(1)} collective-permute-done((bf16[8,2048]{1,0:T(8,128)(2,1)S(1)}, bf16[8,2048]{1,0:T(8,128)(2,1)S(1)}, u32[]{:S(2)}, u32[]{:S(2)}) %collective-permute-start.13) | collective-permute-done | bytes 32800 | tf_op jit(solution)/shard_map/ppermute | solution.py:98
  194.0 6.0 %collective-permute-done.14 = bf16[8,2048]{1,0:T(8,128)(2,1)S(1)} collective-permute-done((bf16[8,2048]{1,0:T(8,128)(2,1)S(1)}, bf16[8,2048]{1,0:T(8,128)(2,1)S(1)}, u32[]{:S(2)}, u32[]{:S(2)}) %collective-permute-start.14) | collective-permute-done | bytes 32800 | tf_op jit(solution)/shard_map/ppermute | solution.py:98
  (101 shorter events, 20.1 us)
Async XLA Ops:
  2.4 0.8 copy-start.6
  29.3 1.2 copy-start.2
  30.0 1.4 copy-start
  31.3 7.6 %copy-start.5 = (bf16[8,2048]{1,0:T(8,128)(2,1)S(1)}, bf16[8,2048]{1,0:T(8,128)(2,1)}, u32[]{:S(2)}) copy-start(bf16[8,2048]{1,0:T(8,128)(2,1)} %param.8) | copy-start | bytes 98308
  34.4 56.5 %all-to-all-start = ((f32[16,1,128]{2,1,0:T(1,128)}), f32[16,1,128]{2,1,0:T(1,128)S(1)}, u32[]{:S(2)}, u32[]{:S(2)}) async-start(f32[16,1,128]{2,1,0:T(1,128)} %reshape.418), calls=%async_computation | async-start | bytes 16384 | tf_op jit(solution)/shard_map/all_to_all | solution.py:75
  37.9 70.3 %collective-permute-start = (bf16[8,2048]{1,0:T(8,128)(2,1)}, bf16[8,2048]{1,0:T(8,128)(2,1)}, u32[]{:S(2)}, u32[]{:S(2)}) collective-permute-start(bf16[8,2048]{1,0:T(8,128)(2,1)} %param.9), channel_id=1, source_target_pairs={{0,1},{1,2},{2,3},{3,4},{4,5},{5,6},{6,7},{7,8},{8,9},{9,10},{10,1... | collective-permute-start | bytes 98312 | tf_op jit(solution)/shard_map/ppermute | solution.py:98
  77.6 3.5 %copy-start.4 = (bf16[16,8,16,128]{3,2,1,0:T(8,128)(2,1)S(1)}, bf16[16,8,16,128]{3,2,1,0:T(8,128)(2,1)}, u32[]{:S(2)}) copy-start(bf16[16,8,16,128]{3,2,1,0:T(8,128)(2,1)} %copy.112) | copy-start | bytes 1572868
  82.9 1.8 copy-start.1
  84.7 4.7 %copy-start.7 = (f32[1,128,16]{1,2,0:T(8,128)S(1)}, f32[1,128,16]{1,2,0:T(8,128)}, u32[]{:S(2)}) copy-start(f32[1,128,16]{1,2,0:T(8,128)} %get-tuple-element.21) | copy-start | bytes 24580
  90.9 10.4 %all-to-all-start.1 = ((f32[16,1,128]{2,1,0:T(1,128)}), f32[16,1,128]{2,1,0:T(1,128)S(1)}, u32[]{:S(2)}, u32[]{:S(2)}) async-start(f32[16,1,128]{2,1,0:T(1,128)} %reshape.422), calls=%async_computation.1 | async-start | bytes 16384 | tf_op jit(solution)/shard_map/all_to_all | solution.py:74
  99.3 100.8 %copy-start.3 = (bf16[8,16,16,8]{0,3,1,2:T(8,128)(2,1)S(1)}, bf16[8,16,16,8]{0,3,1,2:T(8,128)(2,1)}, u32[]{:S(2)}) copy-start(bf16[8,16,16,8]{0,3,1,2:T(8,128)(2,1)} %get-tuple-element.20) | copy-start | bytes 98308
  101.4 99.3 %all-to-all-start.2 = ((bf16[16,2,8192]{2,1,0:T(2,128)(2,1)}), bf16[16,2,8192]{2,1,0:T(2,128)(2,1)S(1)}, u32[]{:S(2)}, u32[]{:S(2)}) async-start(bf16[16,2,8192]{2,1,0:T(2,128)(2,1)} %reshape.420), calls=%async_computation.2 | async-start | bytes 1048576 | tf_op jit(solution)/shard_map/all_to_all | solution.py:66
  108.2 13.3 %collective-permute-start.1 = (bf16[8,2048]{1,0:T(8,128)(2,1)}, bf16[8,2048]{1,0:T(8,128)(2,1)S(1)}, u32[]{:S(2)}, u32[]{:S(2)}) collective-permute-start(bf16[8,2048]{1,0:T(8,128)(2,1)} %collective-permute-done), channel_id=1, source_target_pairs={{0,1},{1,2},{2,3},{3,4},{4,5},{5,6},{6,7},{7,8},{8,9},{9,10},{10,1... | collective-permute-start | bytes 98312 | tf_op jit(solution)/shard_map/ppermute | solution.py:98
  121.6 6.0 %collective-permute-start.2 = (bf16[8,2048]{1,0:T(8,128)(2,1)S(1)}, bf16[8,2048]{1,0:T(8,128)(2,1)S(1)}, u32[]{:S(2)}, u32[]{:S(2)}) collective-permute-start(bf16[8,2048]{1,0:T(8,128)(2,1)S(1)} %collective-permute-done.1), channel_id=1, source_target_pairs={{0,1},{1,2},{2,3},{3,4},{4,5},{5,6},{6,7},{7,8},{8,9},{9,10},{10,1... | collective-permute-start | bytes 98312 | tf_op jit(solution)/shard_map/ppermute | solution.py:98
  127.6 6.0 %collective-permute-start.3 = (bf16[8,2048]{1,0:T(8,128)(2,1)S(1)}, bf16[8,2048]{1,0:T(8,128)(2,1)S(1)}, u32[]{:S(2)}, u32[]{:S(2)}) collective-permute-start(bf16[8,2048]{1,0:T(8,128)(2,1)S(1)} %collective-permute-done.2), channel_id=1, source_target_pairs={{0,1},{1,2},{2,3},{3,4},{4,5},{5,6},{6,7},{7,8},{8,9},{9,10},{10,1... | collective-permute-start | bytes 98312 | tf_op jit(solution)/shard_map/ppermute | solution.py:98
  133.6 6.0 %collective-permute-start.4 = (bf16[8,2048]{1,0:T(8,128)(2,1)S(1)}, bf16[8,2048]{1,0:T(8,128)(2,1)S(1)}, u32[]{:S(2)}, u32[]{:S(2)}) collective-permute-start(bf16[8,2048]{1,0:T(8,128)(2,1)S(1)} %collective-permute-done.3), channel_id=1, source_target_pairs={{0,1},{1,2},{2,3},{3,4},{4,5},{5,6},{6,7},{7,8},{8,9},{9,10},{10,1... | collective-permute-start | bytes 98312 | tf_op jit(solution)/shard_map/ppermute | solution.py:98
  139.7 6.0 %collective-permute-start.5 = (bf16[8,2048]{1,0:T(8,128)(2,1)S(1)}, bf16[8,2048]{1,0:T(8,128)(2,1)S(1)}, u32[]{:S(2)}, u32[]{:S(2)}) collective-permute-start(bf16[8,2048]{1,0:T(8,128)(2,1)S(1)} %collective-permute-done.4), channel_id=1, source_target_pairs={{0,1},{1,2},{2,3},{3,4},{4,5},{5,6},{6,7},{7,8},{8,9},{9,10},{10,1... | collective-permute-start | bytes 98312 | tf_op jit(solution)/shard_map/ppermute | solution.py:98
  145.7 6.0 %collective-permute-start.6 = (bf16[8,2048]{1,0:T(8,128)(2,1)S(1)}, bf16[8,2048]{1,0:T(8,128)(2,1)S(1)}, u32[]{:S(2)}, u32[]{:S(2)}) collective-permute-start(bf16[8,2048]{1,0:T(8,128)(2,1)S(1)} %collective-permute-done.5), channel_id=1, source_target_pairs={{0,1},{1,2},{2,3},{3,4},{4,5},{5,6},{6,7},{7,8},{8,9},{9,10},{10,1... | collective-permute-start | bytes 98312 | tf_op jit(solution)/shard_map/ppermute | solution.py:98
  151.7 6.0 %collective-permute-start.7 = (bf16[8,2048]{1,0:T(8,128)(2,1)S(1)}, bf16[8,2048]{1,0:T(8,128)(2,1)S(1)}, u32[]{:S(2)}, u32[]{:S(2)}) collective-permute-start(bf16[8,2048]{1,0:T(8,128)(2,1)S(1)} %collective-permute-done.6), channel_id=1, source_target_pairs={{0,1},{1,2},{2,3},{3,4},{4,5},{5,6},{6,7},{7,8},{8,9},{9,10},{10,1... | collective-permute-start | bytes 98312 | tf_op jit(solution)/shard_map/ppermute | solution.py:98
  157.8 6.0 %collective-permute-start.8 = (bf16[8,2048]{1,0:T(8,128)(2,1)S(1)}, bf16[8,2048]{1,0:T(8,128)(2,1)S(1)}, u32[]{:S(2)}, u32[]{:S(2)}) collective-permute-start(bf16[8,2048]{1,0:T(8,128)(2,1)S(1)} %collective-permute-done.7), channel_id=1, source_target_pairs={{0,1},{1,2},{2,3},{3,4},{4,5},{5,6},{6,7},{7,8},{8,9},{9,10},{10,1... | collective-permute-start | bytes 98312 | tf_op jit(solution)/shard_map/ppermute | solution.py:98
  163.8 6.0 %collective-permute-start.9 = (bf16[8,2048]{1,0:T(8,128)(2,1)S(1)}, bf16[8,2048]{1,0:T(8,128)(2,1)S(1)}, u32[]{:S(2)}, u32[]{:S(2)}) collective-permute-start(bf16[8,2048]{1,0:T(8,128)(2,1)S(1)} %collective-permute-done.8), channel_id=1, source_target_pairs={{0,1},{1,2},{2,3},{3,4},{4,5},{5,6},{6,7},{7,8},{8,9},{9,10},{10,1... | collective-permute-start | bytes 98312 | tf_op jit(solution)/shard_map/ppermute | solution.py:98
  169.9 6.0 %collective-permute-start.10 = (bf16[8,2048]{1,0:T(8,128)(2,1)S(1)}, bf16[8,2048]{1,0:T(8,128)(2,1)S(1)}, u32[]{:S(2)}, u32[]{:S(2)}) collective-permute-start(bf16[8,2048]{1,0:T(8,128)(2,1)S(1)} %collective-permute-done.9), channel_id=1, source_target_pairs={{0,1},{1,2},{2,3},{3,4},{4,5},{5,6},{6,7},{7,8},{8,9},{9,10},{10,1... | collective-permute-start | bytes 98312 | tf_op jit(solution)/shard_map/ppermute | solution.py:98
  175.9 6.0 %collective-permute-start.11 = (bf16[8,2048]{1,0:T(8,128)(2,1)S(1)}, bf16[8,2048]{1,0:T(8,128)(2,1)S(1)}, u32[]{:S(2)}, u32[]{:S(2)}) collective-permute-start(bf16[8,2048]{1,0:T(8,128)(2,1)S(1)} %collective-permute-done.10), channel_id=1, source_target_pairs={{0,1},{1,2},{2,3},{3,4},{4,5},{5,6},{6,7},{7,8},{8,9},{9,10},{10,1... | collective-permute-start | bytes 98312 | tf_op jit(solution)/shard_map/ppermute | solution.py:98
  181.9 6.0 %collective-permute-start.12 = (bf16[8,2048]{1,0:T(8,128)(2,1)S(1)}, bf16[8,2048]{1,0:T(8,128)(2,1)S(1)}, u32[]{:S(2)}, u32[]{:S(2)}) collective-permute-start(bf16[8,2048]{1,0:T(8,128)(2,1)S(1)} %collective-permute-done.11), channel_id=1, source_target_pairs={{0,1},{1,2},{2,3},{3,4},{4,5},{5,6},{6,7},{7,8},{8,9},{9,10},{10,1... | collective-permute-start | bytes 98312 | tf_op jit(solution)/shard_map/ppermute | solution.py:98
  188.0 6.0 %collective-permute-start.13 = (bf16[8,2048]{1,0:T(8,128)(2,1)S(1)}, bf16[8,2048]{1,0:T(8,128)(2,1)S(1)}, u32[]{:S(2)}, u32[]{:S(2)}) collective-permute-start(bf16[8,2048]{1,0:T(8,128)(2,1)S(1)} %collective-permute-done.12), channel_id=1, source_target_pairs={{0,1},{1,2},{2,3},{3,4},{4,5},{5,6},{6,7},{7,8},{8,9},{9,10},{10,1... | collective-permute-start | bytes 98312 | tf_op jit(solution)/shard_map/ppermute | solution.py:98
  194.0 6.0 %collective-permute-start.14 = (bf16[8,2048]{1,0:T(8,128)(2,1)S(1)}, bf16[8,2048]{1,0:T(8,128)(2,1)S(1)}, u32[]{:S(2)}, u32[]{:S(2)}) collective-permute-start(bf16[8,2048]{1,0:T(8,128)(2,1)S(1)} %collective-permute-done.13), channel_id=1, source_target_pairs={{0,1},{1,2},{2,3},{3,4},{4,5},{5,6},{6,7},{7,8},{8,9},{9,10},{10,1... | collective-permute-start | bytes 98312 | tf_op jit(solution)/shard_map/ppermute | solution.py:98
